TPU v7x, 128 devices: a whole 4x4x4 slice. The times are simulated.
128 devices in a mesh: gx: 4 (over y), gy: 8 (over z, x_lo), gz: 4 (over x_hi, core).
Axes of the slice: x: 4 (x_hi: 2, x_lo: 2; x = x_hi * 2 + x_lo), y: 4, z: 4, core: 2. Of those that a mesh axis runs over, the one named last changes fastest.
Arguments:
- node_latent: bfloat16 [64, 256, 16, 128], P('gx', 'gy', 'gz'), may hold values from -6 to 6
- edge_latent: bfloat16 [4, 8, 4, 12288, 128], P('gx', 'gy', 'gz'), may hold values from -6 to 6
- senders: int32 [4, 8, 4, 12288], P('gx', 'gy', 'gz'), may hold values from 7 to 3664, as said below
- receivers: int32 [4, 8, 4, 12288], P('gx', 'gy', 'gz'), may hold values from 0 to 2047, as said below
- w1_edge: bfloat16 [384, 128], replicated, may hold values from -0.3125 to 0.3125
- b1_edge: float32 [128], replicated, may hold values from -3 to 3
- w2_edge: bfloat16 [128, 128], replicated, may hold values from -0.5 to 0.5
- b2_edge: float32 [128], replicated, may hold values from -3 to 3
- w1_node: bfloat16 [256, 128], replicated, may hold values from -0.375 to 0.375
- b1_node: float32 [128], replicated, may hold values from -3 to 3
- w2_node: bfloat16 [128, 128], replicated, may hold values from -0.5 to 0.5
- cot_node: bfloat16 [64, 256, 16, 128], P('gx', 'gy', 'gz'), may hold values from -6 to 6
- cot_edge: bfloat16 [4, 8, 4, 12288, 128], P('gx', 'gy', 'gz'), may hold values from -8 to 8
Outputs:
- grad_node: bfloat16 [64, 256, 16, 128], P('gx', 'gy', 'gz')
- grad_edge: bfloat16 [4, 8, 4, 12288, 128], P('gx', 'gy', 'gz')
- grad_w1_edge: float32 [384, 128], replicated
- grad_w2_edge: float32 [128, 128], replicated
- grad_w1_node: float32 [256, 128], replicated
- grad_w2_node: float32 [128, 128], replicated
- grad_biases: float32 [4, 128], replicated
Inputs may be any that keep to these rules, and one draw needn't show every extreme that they name: `receivers`: in every block the list is nondecreasing; entry (i * 32 + j) * 4 + l names the block's cell at local coordinates (i, j, l). `senders`: entry (p * 34 + q) * 6 + r names the cell at local coordinates (p - 1, q - 1, r - 1) of the block extended by one cell on every side, the extension being cells of the adjacent blocks around the periodic box; it is always one of the six face neighbours of the same slot's receiver.
All inputs are finite; a program needn't handle non-finite values.
Results may differ from a plain program's by a relative error of at most 0.01.
Values may be sent and summed in bfloat16 or wider, within the bound.
A program may use at most 128 MiB of HBM per device.

v0:
```python
import jax
import jax.numpy as jnp
from jax import lax
from jax.sharding import PartitionSpec as P


def with_halo(shard, sides, width):
    edges = {}
    for axis, dim in sides:
        peers, length = (lax.axis_size(axis), shard.shape[dim])
        up = [(i, (i + 1) % peers) for i in range(peers)]
        last = lax.slice_in_dim(shard, length - width, length, axis=dim)
        leading = lax.slice_in_dim(shard, 0, width, axis=dim)
        edges[dim] = (
            lax.ppermute(last, axis, up),
            lax.ppermute(leading, axis, [(b, a) for a, b in up]),
        )
    done = []
    for _, dim in sides:
        low, high = edges[dim]
        around = [(width, width) if d in done else (0, 0) for d in range(shard.ndim)]
        shard = jnp.concatenate([jnp.pad(low, around), shard, jnp.pad(high, around)], axis=dim)
        done.append(dim)
    return shard


def transposed_dot(left, right):
    return lax.dot_general(
        left, right, (((0,), (0,)), ((), ())), preferred_element_type=jnp.float32
    )


def column_sums(values):
    return jnp.sum(values.astype(jnp.float32), axis=0)


def silu_slope(values):
    sigma = jax.nn.sigmoid(values)
    return sigma * (1.0 + values * (1.0 - sigma))


def reduce_flat(flat_grads):
    return lax.psum(flat_grads, ("gx", "gy", "gz"))


def on_device(
    node_latent,
    edge_latent,
    senders,
    receivers,
    w1_edge,
    b1_edge,
    w2_edge,
    b2_edge,
    w1_node,
    b1_node,
    w2_node,
    cot_node,
    cot_edge,
):
    side_x, side_y, side_z, latent = node_latent.shape
    cell_count = side_x * side_y * side_z
    edge_count = edge_latent.shape[3]
    padded = with_halo(node_latent, (("gx", 0), ("gy", 1), ("gz", 2)), 1)
    flat_pad = padded.reshape(-1, latent)
    own_rows = node_latent.reshape(cell_count, latent)
    edge_rows = edge_latent.reshape(edge_count, latent)
    cot_rows = cot_edge.reshape(edge_count, latent)
    cot_cells = cot_node.reshape(cell_count, latent)
    sender_ids = senders.reshape(edge_count)
    receiver_ids = receivers.reshape(edge_count)
    sender_rows = jnp.take(flat_pad, sender_ids, axis=0)
    receiver_rows = jnp.take(own_rows, receiver_ids, axis=0)
    x_edge = jnp.concatenate([edge_rows, sender_rows, receiver_rows], axis=1)
    z_edge = jnp.dot(x_edge, w1_edge, preferred_element_type=jnp.float32) + b1_edge
    u_edge = jax.nn.silu(z_edge).astype(jnp.bfloat16)
    edge_new = (
        edge_rows.astype(jnp.float32)
        + jnp.dot(u_edge, w2_edge, preferred_element_type=jnp.float32)
        + b2_edge
    ).astype(jnp.bfloat16)
    aggregate = jax.ops.segment_sum(
        edge_new.astype(jnp.float32), receiver_ids, cell_count, indices_are_sorted=True
    ).astype(jnp.bfloat16)
    x_node = jnp.concatenate([own_rows, aggregate], axis=1)
    z_node = jnp.dot(x_node, w1_node, preferred_element_type=jnp.float32) + b1_node
    u_node = jax.nn.silu(z_node).astype(jnp.bfloat16)
    dz_node = (
        jnp.dot(cot_cells, w2_node.T, preferred_element_type=jnp.float32) * silu_slope(z_node)
    ).astype(jnp.bfloat16)
    dx_node = jnp.dot(dz_node, w1_node.T, preferred_element_type=jnp.float32)
    node_flat = jnp.concatenate(
        [
            transposed_dot(x_node, dz_node).reshape(-1),
            column_sums(dz_node),
            transposed_dot(u_node, cot_cells).reshape(-1),
            column_sums(cot_cells),
        ]
    )
    d_edge = (
        cot_rows.astype(jnp.float32) + jnp.take(dx_node[:, latent:], receiver_ids, axis=0)
    ).astype(jnp.bfloat16)
    dz_edge = (
        jnp.dot(d_edge, w2_edge.T, preferred_element_type=jnp.float32) * silu_slope(z_edge)
    ).astype(jnp.bfloat16)
    d_self = jnp.dot(dz_edge, w1_edge[:latent].T, preferred_element_type=jnp.float32)
    d_sender = jnp.dot(dz_edge, w1_edge[latent : 2 * latent].T, preferred_element_type=jnp.float32)
    d_receiver = jnp.dot(dz_edge, w1_edge[2 * latent :].T, preferred_element_type=jnp.float32)
    grad_edge = (
        (d_edge.astype(jnp.float32) + d_self).astype(jnp.bfloat16).reshape(edge_latent.shape)
    )
    edge_flat = jnp.concatenate(
        [
            transposed_dot(x_edge, dz_edge).reshape(-1),
            column_sums(dz_edge),
            transposed_dot(u_edge, d_edge).reshape(-1),
            column_sums(d_edge),
        ]
    )
    summed = (reduce_flat(jnp.concatenate([node_flat, edge_flat])),)
    send_grid = jax.ops.segment_sum(d_sender, sender_ids, flat_pad.shape[0]).reshape(
        side_x + 2, side_y + 2, side_z + 2, latent
    )
    receiver_sum = jax.ops.segment_sum(
        d_receiver, receiver_ids, cell_count, indices_are_sorted=True
    )
    own_terms = cot_cells.astype(jnp.float32) + dx_node[:, :latent] + receiver_sum
    interior = send_grid[1:-1, 1:-1, 1:-1] + own_terms.reshape(side_x, side_y, side_z, latent)
    extended = with_halo(
        send_grid.astype(jnp.bfloat16), (("gx", 0), ("gy", 1), ("gz", 2)), 1
    ).astype(send_grid.dtype)
    interior = interior.at[0].add(extended[0, 2:-2, 2:-2]).at[-1].add(extended[-1, 2:-2, 2:-2])
    interior = (
        interior.at[:, 0].add(extended[2:-2, 0, 2:-2]).at[:, -1].add(extended[2:-2, -1, 2:-2])
    )
    interior = (
        interior.at[:, :, 0].add(extended[2:-2, 2:-2, 0]).at[:, :, -1].add(extended[2:-2, 2:-2, -1])
    )
    grad_node = interior.astype(jnp.bfloat16)
    param_count = 7 * latent * latent + 4 * latent
    partial_value = sum((jnp.sum(portion * portion) for portion in summed))
    factor = 1.0 / jnp.maximum(1.0, jnp.sqrt(partial_value / param_count))
    scaled = [portion * factor for portion in summed]
    full_grads = scaled[0]
    square = latent * latent
    cut_a = 2 * square
    cut_b = cut_a + latent
    cut_c = cut_b + square
    cut_d = cut_c + latent
    cut_e = cut_d + 3 * square
    cut_f = cut_e + latent
    cut_g = cut_f + square
    grad_w1_node = full_grads[:cut_a].reshape(2 * latent, latent)
    bias_one_node = full_grads[cut_a:cut_b]
    grad_w2_node = full_grads[cut_b:cut_c].reshape(latent, latent)
    bias_two_node = full_grads[cut_c:cut_d]
    grad_w1_edge = full_grads[cut_d:cut_e].reshape(3 * latent, latent)
    bias_one_edge = full_grads[cut_e:cut_f]
    grad_w2_edge = full_grads[cut_f:cut_g].reshape(latent, latent)
    bias_two_edge = full_grads[cut_g:]
    grad_biases = jnp.stack([bias_one_edge, bias_two_edge, bias_one_node, bias_two_node])
    return (
        grad_node,
        grad_edge,
        grad_w1_edge,
        grad_w2_edge,
        grad_w1_node,
        grad_w2_node,
        grad_biases,
    )


def solution(mesh):
    placed = (
        P("gx", "gy", "gz", None),
        P("gx", "gy", "gz", None, None),
        P("gx", "gy", "gz", None),
        P("gx", "gy", "gz", None),
        P(),
        P(),
        P(),
        P(),
        P(),
        P(),
        P(),
        P("gx", "gy", "gz", None),
        P("gx", "gy", "gz", None, None),
    )
    return jax.shard_map(
        on_device,
        mesh=mesh,
        in_specs=placed,
        out_specs=(
            P("gx", "gy", "gz", None),
            P("gx", "gy", "gz", None, None),
            P(),
            P(),
            P(),
            P(),
            P(),
        ),
        check_vma=False,
    )
```

profile of v0, /device:TPU:1, one launch (start us, length us, event | category | flops | bytes accessed | tf_op | source)
XLA Modules:
  0.0 521.8 jit_solution(16961521660698633385)
XLA Ops:
  7.2 0.8 fusion.63
  8.1 2.1 collective-permute-start.1
  10.2 3.6 collective-permute-start.4
  14.5 1.4 collective-permute-start.2
  15.9 1.5 collective-permute-start.3
  17.4 1.8 fusion.62
  19.2 3.8 collective-permute-start
  22.9 0.8 compare_select_fusion
  23.8 0.8 compare_and_fusion.1
  24.6 0.9 compare_select_fusion.1
  25.5 0.8 compare_and_fusion
  26.4 1.6 convert_reduce_fusion.2
  28.0 43.3 %gather_fusion.1 = bf16[12288,128]{1,0:T(8,128)(2,1)} fusion(bf16[2048,128]{1,0:T(8,128)(2,1)S(1)} %bitcast.62, s32[12288]{0:T(1024)S(1)} %broadcast_clamp_fusion), kind=kCustom, calls=%fused_computation.1 | custom fusion | bytes 6340608 | tf_op jit(solution)/shard_map/jit(_take)/gather | solution.py:73
  71.4 2.1 fusion.34
  73.8 43.7 %gather_fusion = bf16[12288,128]{1,0:T(8,128)(2,1)} fusion(bf16[3672,128]{1,0:T(8,128)(2,1)S(1)} %reshape.366, s32[12288]{0:T(1024)S(1)} %broadcast_clamp_fusion.1), kind=kCustom, calls=%fused_computation | custom fusion | bytes 6340608 | tf_op jit(solution)/shard_map/jit(_take)/gather | solution.py:72
  117.5 9.2 %broadcast_select_fusion = (bf16[12288,128]{1,0:T(8,128)(2,1)S(1)}, bf16[12288,128]{1,0:T(8,128)(2,1)S(1)}) fusion(bf16[12288,128]{1,0:T(8,128)(2,1)} %gather_fusion, pred[12288]{0:T(1024)(128)(4,1)S(1)} %compare_and_fusion, bf16[12288,128]{1,0:T(8,128)(2,1)} %gather_fusion.1, pred[12288]{0:T(1024)(128)(4,1)S(1)} %compare_and_fusion.1), kind=kLoop, calls=%fused_computation.38 | loop fusion | flops 3145728 | bytes 12607488 | tf_op jit(solution)/shard_map/jit(_take)/select_n | solution.py:72
  126.8 3.0 convolution_add_fusion.2
  129.8 2.6 copy-done.25
  132.5 3.8 fusion.4
  136.3 76.0 %scatter_custom_fusion = f32[2048,128]{1,0:T(8,128)S(1)} fusion(s32[12288]{0:T(1024)S(1)} %bitcast.69, f32[12288,128]{1,0:T(8,128)} %fusion.4, f32[]{:T(128)} %constant.207.clone.1), kind=kCustom, calls=%fused_computation.83 | custom fusion | flops 1572864 | bytes 1049088 | tf_op jit(solution)/shard_map/scatter-add | solution.py:82
  212.9 1.1 convolution_bitcast_fusion.3
  215.6 41.2 %gather_fusion.2 = f32[12288,128]{1,0:T(8,128)} fusion(f32[2048,128]{1,0:T(8,128)S(1)} %get-tuple-element.81, s32[12288]{0:T(1024)S(1)} %broadcast_clamp_fusion), kind=kCustom, calls=%fused_computation.2 | custom fusion | bytes 12632064 | tf_op jit(solution)/shard_map/jit(_take)/gather | solution.py:101
  256.8 9.3 %convert_reduce_fusion = (f32[128]{0:T(128)S(1)}, bf16[12288,128]{1,0:T(8,128)(2,1)S(1)}) fusion(f32[12288,128]{1,0:T(8,128)} %gather_fusion.2, pred[12288]{0:T(1024)(128)(4,1)S(1)} %compare_and_fusion.1, bf16[1,1,1,12288,128]{4,3,2,1,0:T(8,128)(2,1)} %param.37), kind=kLoop, calls=%fused_computation.17 | loop fusion | flops 9437056 | bytes 12595712 | tf_op jit(solution)/shard_map/reduce_sum | solution.py:34
  266.1 5.4 %convolution_bitcast_fusion.2 = f32[16384]{0:T(1024)} fusion(bf16[12288,128]{1,0:T(8,128)(2,1)S(1)} %get-tuple-element.80, f32[12288,128]{1,0:T(8,128)} %copy-done.25), kind=kOutput, calls=%fused_computation.63 | convolution fusion | flops 410517504 | bytes 9502720 | tf_op jit(solution)/shard_map/dot_general | solution.py:28
  271.6 3.2 convert_reduce_fusion.1
  275.3 3.3 convolution_bitcast_fusion
  278.6 2.6 fusion.5
  281.3 3.6 fusion.47
  284.9 3.6 fusion.49
  288.5 66.6 %scatter_custom_fusion.1 = f32[3672,128]{1,0:T(8,128)S(1)} fusion(s32[12288]{0:T(1024)} %bitcast.74, f32[12288,128]{1,0:T(8,128)} %fusion.49, f32[]{:T(128)} %constant.207.clone.1), kind=kCustom, calls=%fused_computation.81 | custom fusion | flops 1572864 | bytes 1880576 | tf_op jit(solution)/shard_map/scatter-add | solution.py:121
  355.1 1.7 reshape.367
  356.9 2.0 convert_element_type.85
  359.5 1.3 fusion.59
  361.8 3.6 collective-permute-start.10
  365.5 2.6 collective-permute-start.9
  368.1 4.4 collective-permute-start.6
  372.5 76.1 %scatter_fusion = f32[2048,128]{1,0:T(8,128)S(1)} fusion(f32[2048,128]{1,0:T(8,128)S(1)} %get-tuple-element.82, s32[12288]{0:T(1024)S(1)} %bitcast.70, f32[12288,128]{1,0:T(8,128)} %fusion.47), kind=kCustom, calls=%fused_computation.5 | custom fusion | flops 1572864 | bytes 18923520 | tf_op jit(solution)/shard_map/scatter-add | solution.py:124
  449.3 2.0 slice_add_fusion.1
  451.4 5.5 %collective-permute-done.11 = bf16[18,34,1,128]{3,2,1,0:T(2,128)(2,1)S(1)} collective-permute-done((bf16[18,34,1,128]{3,2,1,0:T(2,128)(2,1)}, bf16[18,34,1,128]{3,2,1,0:T(2,128)(2,1)S(1)}, u32[]{:S(2)}, u32[]{:S(2)}) %collective-permute-start.11) | collective-permute-done | bytes 156704 | tf_op jit(solution)/shard_map/ppermute | solution.py:16
  456.8 3.4 fusion.30
  460.4 1.4 copy-done.3
  462.2 5.3 %scatter-add.58 = f32[16,32,4,128]{3,2,1,0:T(4,128)S(1)} dynamic-update-slice(f32[16,32,4,128]{3,2,1,0:T(4,128)S(1)} %fusion.44, f32[16,32,1,128]{3,2,1,0:T(1,128)S(1)} %slice_add_fusion.3, s32[]{:T(128)} %constant.208.clone.1, s32[]{:T(128)} %constant.208.clone.1, s32[]{:T(128)} %constant.208.clone.1, s32[]{:T(128)} %constant.208.clone.1) | dynamic-update-slice | bytes 524292 | tf_op jit(solution)/shard_map/scatter-add | solution.py:137
  467.4 2.1 slice_add_fusion.2
  469.5 5.3 %scatter-add.59 = f32[16,32,4,128]{3,2,1,0:T(4,128)S(1)} dynamic-update-slice(f32[16,32,4,128]{3,2,1,0:T(4,128)S(1)} %scatter-add.58, f32[16,32,1,128]{3,2,1,0:T(1,128)S(1)} %slice_add_fusion.2, s32[]{:T(128)} %constant.208.clone.1, s32[]{:T(128)} %constant.208.clone.1, s32[]{:T(128)} %constant.219.clone.1, s32[]{:T(128)} %constant.208.clone.1) | dynamic-update-slice | bytes 524292 | tf_op jit(solution)/shard_map/scatter-add | solution.py:137
  474.8 1.0 convert_element_type.87
  475.8 33.0 %all-reduce.10.cloned.1.call-done = f32[115200]{0:T(1024)} async-done(((f32[115200]{0:T(1024)}), f32[115200]{0:T(1024)}) %all-reduce.10.cloned.1.call-update) | async-done | bytes 460816 | tf_op jit(solution)/shard_map/psum | solution.py:43
  508.8 1.7 multiply_reduce_fusion
  511.3 1.1 broadcast_multiply_fusion
  (101 shorter events, 9.4 us)
Async XLA Ops:
  7.2 205.2 %copy-start = (bf16[256,128]{1,0:T(8,128)(2,1)S(1)}, bf16[256,128]{1,0:T(8,128)(2,1)}, u32[]{:S(2)}) copy-start(bf16[256,128]{1,0:T(8,128)(2,1)} %param.33) | copy-start | bytes 196612
  7.2 20.8 %copy-start.2 = (bf16[16,32,4,128]{3,2,1,0:T(4,128)(2,1)S(1)}, bf16[16,32,4,128]{3,2,1,0:T(4,128)(2,1)}, u32[]{:S(2)}) copy-start(bf16[16,32,4,128]{3,2,1,0:T(4,128)(2,1)} %param.25) | copy-start | bytes 1572868
  7.2 501.6 %all-reduce.10.cloned.1.call-start = ((), (), s32[]{:S(2)}) async-start(), calls=%async_computation | async-start | bytes 925696 | tf_op jit(solution)/shard_map/psum | solution.py:43
  8.1 18.3 %collective-permute-start.1 = (bf16[16,1,4,128]{3,2,1,0:T(4,128)(2,1)S(1)}, bf16[16,1,4,128]{3,2,1,0:T(4,128)(2,1)S(1)}, u32[]{:S(2)}, u32[]{:S(2)}) collective-permute-start(bf16[16,1,4,128]{3,2,1,0:T(4,128)(2,1)S(1)} %get-tuple-element.93), channel_id=1, source_target_pairs={{0,4},{4,8},{8,12},{12,16},{16,20},{20,24},{24,28},{28,0},{1,5},{5... | collective-permute-start | bytes 49160 | tf_op jit(solution)/shard_map/ppermute | solution.py:15
  10.2 61.2 %collective-permute-start.4 = (bf16[16,1,4,128]{3,2,1,0:T(4,128)(2,1)S(1)}, bf16[16,1,4,128]{3,2,1,0:T(4,128)(2,1)S(1)}, u32[]{:S(2)}, u32[]{:S(2)}) collective-permute-start(bf16[16,1,4,128]{3,2,1,0:T(4,128)(2,1)S(1)} %get-tuple-element.94), channel_id=1, source_target_pairs={{4,0},{8,4},{12,8},{16,12},{20,16},{24,20},{28,24},{0,28},{5,1},{9... | collective-permute-start | bytes 49160 | tf_op jit(solution)/shard_map/ppermute | solution.py:16
  14.5 56.8 %collective-permute-start.2 = (bf16[1,32,4,128]{3,2,1,0:T(4,128)(2,1)S(1)}, bf16[1,32,4,128]{3,2,1,0:T(4,128)(2,1)S(1)}, u32[]{:S(2)}, u32[]{:S(2)}) collective-permute-start(bf16[1,32,4,128]{3,2,1,0:T(4,128)(2,1)S(1)} %get-tuple-element.89), channel_id=1, source_target_pairs={{0,32},{32,64},{64,96},{96,0},{1,33},{33,65},{65,97},{97,1},{2,34}... | collective-permute-start | bytes 98312 | tf_op jit(solution)/shard_map/ppermute | solution.py:15
  15.9 55.5 %collective-permute-start.3 = (bf16[1,32,4,128]{3,2,1,0:T(4,128)(2,1)S(1)}, bf16[1,32,4,128]{3,2,1,0:T(4,128)(2,1)S(1)}, u32[]{:S(2)}, u32[]{:S(2)}) collective-permute-start(bf16[1,32,4,128]{3,2,1,0:T(4,128)(2,1)S(1)} %get-tuple-element.90), channel_id=1, source_target_pairs={{32,0},{64,32},{96,64},{0,96},{33,1},{65,33},{97,65},{1,97},{34,2}... | collective-permute-start | bytes 98312 | tf_op jit(solution)/shard_map/ppermute | solution.py:16
  19.2 52.2 %collective-permute-start = (bf16[16,32,1,128]{3,2,1,0:T(2,128)(2,1)S(1)}, bf16[16,32,1,128]{3,2,1,0:T(2,128)(2,1)S(1)}, u32[]{:S(2)}, u32[]{:S(2)}) collective-permute-start(bf16[16,32,1,128]{3,2,1,0:T(2,128)(2,1)S(1)} %get-tuple-element.91), channel_id=1, source_target_pairs={{0,1},{1,2},{2,3},{3,0},{4,5},{5,6},{6,7},{7,4},{8,9},{9,10},{10,1... | collective-permute-start | bytes 393224 | tf_op jit(solution)/shard_map/ppermute | solution.py:15
  26.3 45.0 %collective-permute-start.5 = (bf16[16,32,1,128]{3,2,1,0:T(2,128)(2,1)S(1)}, bf16[16,32,1,128]{3,2,1,0:T(2,128)(2,1)S(1)}, u32[]{:S(2)}, u32[]{:S(2)}) collective-permute-start(bf16[16,32,1,128]{3,2,1,0:T(2,128)(2,1)S(1)} %get-tuple-element.92), channel_id=1, source_target_pairs={{1,0},{2,1},{3,2},{0,3},{5,4},{6,5},{7,6},{4,7},{9,8},{10,9},{11,1... | collective-permute-start | bytes 393224 | tf_op jit(solution)/shard_map/ppermute | solution.py:16
  117.5 9.3 %copy-start.12 = (bf16[384,128]{1,0:T(8,128)(2,1)S(1)}, bf16[384,128]{1,0:T(8,128)(2,1)}, u32[]{:S(2)}) copy-start(bf16[384,128]{1,0:T(8,128)(2,1)} %param.29) | copy-start | bytes 294916
  117.5 9.3 %copy-start.17 = (bf16[1,1,1,12288,128]{4,3,2,1,0:T(8,128)(2,1)S(1)}, bf16[1,1,1,12288,128]{4,3,2,1,0:T(8,128)(2,1)}, u32[]{:S(2)}) copy-start(bf16[1,1,1,12288,128]{4,3,2,1,0:T(8,128)(2,1)} %param.26) | copy-start | bytes 9437188
  117.5 9.3 %copy-start.21 = (f32[128]{0:T(128)S(1)}, f32[128]{0:T(128)}, u32[]{:S(2)}) copy-start(f32[128]{0:T(128)} %param.30) | copy-start | bytes 1540
  126.8 3.1 copy-start.4
  126.8 3.1 copy-start.6
  126.8 5.7 %copy-start.20 = (bf16[128,128]{1,0:T(8,128)(2,1)S(1)}, bf16[128,128]{1,0:T(8,128)(2,1)}, u32[]{:S(2)}) copy-start(bf16[128,128]{1,0:T(8,128)(2,1)} %param.31) | copy-start | bytes 98308
  126.8 5.7 %copy-start.22 = (f32[128]{0:T(128)S(1)}, f32[128]{0:T(128)}, u32[]{:S(2)}) copy-start(f32[128]{0:T(128)} %param.32) | copy-start | bytes 1540
  129.8 2.6 copy-start.25
  132.5 3.8 copy-start.10
  132.5 79.9 %copy-start.23 = (f32[128]{0:T(128)S(1)}, f32[128]{0:T(128)}, u32[]{:S(2)}) copy-start(f32[128]{0:T(128)} %param.34) | copy-start | bytes 1540
  136.3 76.6 %copy-start.8 = (bf16[16,32,4,128]{3,2,1,0:T(4,128)(2,1)S(1)}, bf16[16,32,4,128]{3,2,1,0:T(4,128)(2,1)}, u32[]{:S(2)}) copy-start(bf16[16,32,4,128]{3,2,1,0:T(4,128)(2,1)} %param.36) | copy-start | bytes 1572868
  212.4 1.6 copy-start.19
  256.8 14.7 %slice-start = ((s8[6291456]{0:T(1024)(128)(4,1)}), s8[4194304]{0:T(1024)(128)(4,1)S(1)}, s32[]{:S(2)}) async-start(s8[6291456]{0:T(1024)(128)(4,1)} %bitcast.77), calls=%async_computation.1 | async-start | bytes 8388608
  266.1 5.5 %slice-start.1 = ((s8[6291456]{0:T(1024)(128)(4,1)}), s8[2097152]{0:T(1024)(128)(4,1)S(1)}, s32[]{:S(2)}) async-start(s8[6291456]{0:T(1024)(128)(4,1)} %bitcast.77), calls=%async_computation.2 | async-start | bytes 4194304
  271.6 3.3 copy-start.5
  271.6 3.3 copy-start.7
  271.6 3.7 copy-start.18
  356.8 3.9 copy-start.13
  356.8 4.0 copy-start.11
  356.8 4.1 copy-start.24
  356.8 4.1 copy-start.14
  360.8 87.9 %collective-permute-start.7 = (bf16[18,1,6,128]{3,2,1,0:T(8,128)(2,1)S(1)}, bf16[18,1,6,128]{3,2,1,0:T(8,128)(2,1)S(1)}, u32[]{:S(2)}, u32[]{:S(2)}) collective-permute-start(bf16[18,1,6,128]{3,2,1,0:T(8,128)(2,1)S(1)} %get-tuple-element.87), channel_id=1, source_target_pairs={{0,4},{4,8},{8,12},{12,16},{16,20},{20,24},{24,28},{28,0},{1,5},{5... | collective-permute-start | bytes 82952 | tf_op jit(solution)/shard_map/ppermute | solution.py:15
  361.0 0.8 copy-start.9
  361.8 89.5 %collective-permute-start.10 = (bf16[18,1,6,128]{3,2,1,0:T(8,128)(2,1)S(1)}, bf16[18,1,6,128]{3,2,1,0:T(8,128)(2,1)S(1)}, u32[]{:S(2)}, u32[]{:S(2)}) collective-permute-start(bf16[18,1,6,128]{3,2,1,0:T(8,128)(2,1)S(1)} %get-tuple-element.88), channel_id=1, source_target_pairs={{4,0},{8,4},{12,8},{16,12},{20,16},{24,20},{28,24},{0,28},{5,1},{9... | collective-permute-start | bytes 82952 | tf_op jit(solution)/shard_map/ppermute | solution.py:16
  365.4 85.9 %collective-permute-start.8 = (bf16[1,34,6,128]{3,2,1,0:T(8,128)(2,1)}, bf16[1,34,6,128]{3,2,1,0:T(8,128)(2,1)}, u32[]{:S(2)}, u32[]{:S(2)}) collective-permute-start(bf16[1,34,6,128]{3,2,1,0:T(8,128)(2,1)} %get-tuple-element.83), channel_id=1, source_target_pairs={{0,32},{32,64},{64,96},{96,0},{1,33},{33,65},{65,97},{97,1},{2,34}... | collective-permute-start | bytes 156680 | tf_op jit(solution)/shard_map/ppermute | solution.py:15
  365.5 85.8 %collective-permute-start.9 = (bf16[1,34,6,128]{3,2,1,0:T(8,128)(2,1)}, bf16[1,34,6,128]{3,2,1,0:T(8,128)(2,1)}, u32[]{:S(2)}, u32[]{:S(2)}) collective-permute-start(bf16[1,34,6,128]{3,2,1,0:T(8,128)(2,1)} %get-tuple-element.84), channel_id=1, source_target_pairs={{32,0},{64,32},{96,64},{0,96},{33,1},{65,33},{97,65},{1,97},{34,2}... | collective-permute-start | bytes 156680 | tf_op jit(solution)/shard_map/ppermute | solution.py:16
  368.1 83.3 %collective-permute-start.6 = (bf16[18,34,1,128]{3,2,1,0:T(2,128)(2,1)}, bf16[18,34,1,128]{3,2,1,0:T(2,128)(2,1)}, u32[]{:S(2)}, u32[]{:S(2)}) collective-permute-start(bf16[18,34,1,128]{3,2,1,0:T(2,128)(2,1)} %get-tuple-element.85), channel_id=1, source_target_pairs={{0,1},{1,2},{2,3},{3,0},{4,5},{5,6},{6,7},{7,4},{8,9},{9,10},{10,1... | collective-permute-start | bytes 470024 | tf_op jit(solution)/shard_map/ppermute | solution.py:15
  448.7 0.6 copy-start.15
  448.7 8.1 %collective-permute-start.11 = (bf16[18,34,1,128]{3,2,1,0:T(2,128)(2,1)}, bf16[18,34,1,128]{3,2,1,0:T(2,128)(2,1)S(1)}, u32[]{:S(2)}, u32[]{:S(2)}) collective-permute-start(bf16[18,34,1,128]{3,2,1,0:T(2,128)(2,1)} %get-tuple-element.86), channel_id=1, source_target_pairs={{1,0},{2,1},{3,2},{0,3},{5,4},{6,5},{7,6},{4,7},{9,8},{10,9},{11,1... | collective-permute-start | bytes 470024 | tf_op jit(solution)/shard_map/ppermute | solution.py:16
  449.3 7.5 %copy-start.16 = (bf16[18,1,6,128]{3,2,1,0:T(8,128)(2,1)S(1)}, bf16[18,1,6,128]{3,2,1,0:T(8,128)(2,1)}, u32[]{:S(2)}) copy-start(bf16[18,1,6,128]{3,2,1,0:T(8,128)(2,1)} %copy-done.15) | copy-start | bytes 82948
  460.2 1.6 copy-start.3
  460.3 54.6 %copy-start.1 = (bf16[256,128]{1,0:T(8,128)(2,1)S(1)}, bf16[256,128]{1,0:T(8,128)(2,1)}, u32[]{:S(2)}) copy-start(bf16[256,128]{1,0:T(8,128)(2,1)} %param.33) | copy-start | bytes 196612
Sparse Core Ops, SparseCore 0:
  361.9 146.8 all-reduce.9
where the time goes:
time: 523 us; the launch traced here: 522 us
  other arithmetic  259 us (50%)
  local copies, waits for them, and re-layouts  154 us (29%)
  waiting for transfers between devices  38.5 us (7%)
  matrix products  31.6 us (6%)
  starting transfers between devices  23.2 us (4%)
  between operations  15.3 us (3%)
    scatter-add x1, other arithmetic, on_device(): jax.ops.segment_sum(d_receiver, receiver_ids, cell_count, indices_are_sor...  76.1 us
    scatter-add x1, other arithmetic, on_device(): jax.ops.segment_sum(edge_new.astype(jnp.float32), receiver_ids, cell_coun...  76 us
    scatter-add x1, other arithmetic, on_device(): jax.ops.segment_sum(d_sender, sender_ids, flat_pad.shape[0])  66.6 us
    gather x1, local copies, waits for them, and re-layouts, on_device(): sender_rows = jnp.take(flat_pad, sender_ids, axis=0)  43.7 us
    gather x1, local copies, waits for them, and re-layouts, on_device(): receiver_rows = jnp.take(own_rows, receiver_ids, axis=0)  43.3 us
    gather x1, local copies, waits for them, and re-layouts, on_device(): jnp.take(dx_node[:, latent:], receiver_ids, axis=0)  41.2 us
    psum x1, waiting for transfers between devices, reduce_flat(): return lax.psum(flat_grads, ('gx', 'gy', 'gz'))  33 us
    ppermute x6, starting transfers between devices, with_halo(): lax.ppermute(last, axis, up)  11.8 us
  transfers between devices with their start and end apart: 13, of which 2 were waited for; matrix products, arithmetic and copies ran while one was open for 28% of the time, Pallas kernels for 0%

commit v1 on v0

--- a/solution.py
+++ b/solution.py
@@ -40,7 +40,7 @@
 
 
 def reduce_flat(flat_grads):
-    return lax.psum(flat_grads, ("gx", "gy", "gz"))
+    return lax.psum(lax.psum(flat_grads, ("gy", "gz")), "gx")
 
 
 def on_device(

time: 523 us -> 526 us (level)
    psum x1 -> x2, waiting for transfers between devices: 33 us -> 32.6 us  [reduce_flat(): return lax.psum(lax.psum(flat_grads, ('gy', 'gz')), 'gx')]
  transfers between devices with their start and end apart: 13 -> 14, of which waited for: 2 -> 3; matrix products, arithmetic and copies ran while one was open for 28% -> 28% of each run, Pallas kernels for 0% -> 0%
where the time goes in v1:
time: 526 us; the launch traced here: 523 us
  other arithmetic  260 us (49%)
  local copies, waits for them, and re-layouts  154 us (29%)
  waiting for transfers between devices  38.2 us (7%)
  matrix products  31.6 us (6%)
  starting transfers between devices  23.3 us (4%)
  between operations  15.3 us (3%)
    scatter-add x1, other arithmetic, on_device(): jax.ops.segment_sum(d_receiver, receiver_ids, cell_count, indices_are_sor...  76.1 us
    scatter-add x1, other arithmetic, on_device(): jax.ops.segment_sum(edge_new.astype(jnp.float32), receiver_ids, cell_coun...  76 us
    scatter-add x1, other arithmetic, on_device(): jax.ops.segment_sum(d_sender, sender_ids, flat_pad.shape[0])  66.6 us
    gather x1, local copies, waits for them, and re-layouts, on_device(): sender_rows = jnp.take(flat_pad, sender_ids, axis=0)  43.7 us
    gather x1, local copies, waits for them, and re-layouts, on_device(): receiver_rows = jnp.take(own_rows, receiver_ids, axis=0)  43.3 us
    gather x1, local copies, waits for them, and re-layouts, on_device(): jnp.take(dx_node[:, latent:], receiver_ids, axis=0)  41.2 us
    psum x2, waiting for transfers between devices, reduce_flat(): return lax.psum(lax.psum(flat_grads, ('gy', 'gz')), 'gx')  32.6 us
    ppermute x6, starting transfers between devices, with_halo(): lax.ppermute(last, axis, up)  11.8 us
  transfers between devices with their start and end apart: 14, of which 3 were waited for; matrix products, arithmetic and copies ran while one was open for 28% of the time, Pallas kernels for 0%

profile of v1, /device:TPU:1, one launch (start us, length us, event | category | flops | bytes accessed | tf_op | source)
XLA Modules:
  0.0 523.2 jit_solution(10501172493547226681)
XLA Ops:
  8.1 2.1 collective-permute-start.1
  10.2 3.6 collective-permute-start.4
  14.5 1.4 collective-permute-start.2
  15.9 1.5 collective-permute-start.3
  17.4 1.8 fusion.62
  19.2 3.8 collective-permute-start
  22.9 0.8 compare_select_fusion
  23.8 0.8 compare_and_fusion.1
  24.6 0.9 compare_select_fusion.1
  26.4 1.6 convert_reduce_fusion.2
  28.0 43.3 %gather_fusion.1 = bf16[12288,128]{1,0:T(8,128)(2,1)} fusion(bf16[2048,128]{1,0:T(8,128)(2,1)S(1)} %bitcast.62, s32[12288]{0:T(1024)S(1)} %broadcast_clamp_fusion), kind=kCustom, calls=%fused_computation.1 | custom fusion | bytes 6340608 | tf_op jit(solution)/shard_map/jit(_take)/gather | solution.py:73
  71.4 2.1 fusion.34
  73.8 43.7 %gather_fusion = bf16[12288,128]{1,0:T(8,128)(2,1)} fusion(bf16[3672,128]{1,0:T(8,128)(2,1)S(1)} %reshape.366, s32[12288]{0:T(1024)S(1)} %broadcast_clamp_fusion.1), kind=kCustom, calls=%fused_computation | custom fusion | bytes 6340608 | tf_op jit(solution)/shard_map/jit(_take)/gather | solution.py:72
  117.5 9.2 %broadcast_select_fusion = (bf16[12288,128]{1,0:T(8,128)(2,1)S(1)}, bf16[12288,128]{1,0:T(8,128)(2,1)S(1)}) fusion(bf16[12288,128]{1,0:T(8,128)(2,1)} %gather_fusion, pred[12288]{0:T(1024)(128)(4,1)S(1)} %compare_and_fusion, bf16[12288,128]{1,0:T(8,128)(2,1)} %gather_fusion.1, pred[12288]{0:T(1024)(128)(4,1)S(1)} %compare_and_fusion.1), kind=kLoop, calls=%fused_computation.38 | loop fusion | flops 3145728 | bytes 12607488 | tf_op jit(solution)/shard_map/jit(_take)/select_n | solution.py:72
  126.8 3.0 convolution_add_fusion.2
  129.8 2.6 copy-done.25
  132.5 3.8 fusion.4
  136.3 76.0 %scatter_custom_fusion = f32[2048,128]{1,0:T(8,128)S(1)} fusion(s32[12288]{0:T(1024)S(1)} %bitcast.69, f32[12288,128]{1,0:T(8,128)} %fusion.4, f32[]{:T(128)} %constant.207.clone.1), kind=kCustom, calls=%fused_computation.83 | custom fusion | flops 1572864 | bytes 1049088 | tf_op jit(solution)/shard_map/scatter-add | solution.py:82
  212.9 1.1 convolution_bitcast_fusion.3
  215.6 41.2 %gather_fusion.2 = f32[12288,128]{1,0:T(8,128)} fusion(f32[2048,128]{1,0:T(8,128)S(1)} %get-tuple-element.81, s32[12288]{0:T(1024)S(1)} %broadcast_clamp_fusion), kind=kCustom, calls=%fused_computation.2 | custom fusion | bytes 12632064 | tf_op jit(solution)/shard_map/jit(_take)/gather | solution.py:101
  256.8 9.3 %convert_reduce_fusion = (f32[128]{0:T(128)S(1)}, bf16[12288,128]{1,0:T(8,128)(2,1)S(1)}) fusion(f32[12288,128]{1,0:T(8,128)} %gather_fusion.2, pred[12288]{0:T(1024)(128)(4,1)S(1)} %compare_and_fusion.1, bf16[1,1,1,12288,128]{4,3,2,1,0:T(8,128)(2,1)} %param.37), kind=kLoop, calls=%fused_computation.17 | loop fusion | flops 9437056 | bytes 12595712 | tf_op jit(solution)/shard_map/reduce_sum | solution.py:34
  266.1 5.4 %convolution_bitcast_fusion.2 = f32[16384]{0:T(1024)} fusion(bf16[12288,128]{1,0:T(8,128)(2,1)S(1)} %get-tuple-element.80, f32[12288,128]{1,0:T(8,128)} %copy-done.25), kind=kOutput, calls=%fused_computation.63 | convolution fusion | flops 410517504 | bytes 9502720 | tf_op jit(solution)/shard_map/dot_general | solution.py:28
  271.6 3.2 convert_reduce_fusion.1
  275.3 3.3 convolution_bitcast_fusion
  278.6 2.6 fusion.5
  281.3 3.6 fusion.47
  284.9 3.6 fusion.49
  288.5 66.6 %scatter_custom_fusion.1 = f32[3672,128]{1,0:T(8,128)S(1)} fusion(s32[12288]{0:T(1024)} %bitcast.74, f32[12288,128]{1,0:T(8,128)} %fusion.49, f32[]{:T(128)} %constant.207.clone.1), kind=kCustom, calls=%fused_computation.81 | custom fusion | flops 1572864 | bytes 1880576 | tf_op jit(solution)/shard_map/scatter-add | solution.py:121
  355.1 1.7 reshape.367
  356.9 2.0 convert_element_type.85
  359.5 1.3 fusion.59
  361.8 3.6 collective-permute-start.10
  365.6 2.6 collective-permute-start.9
  368.1 4.4 collective-permute-start.6
  372.5 76.1 %scatter_fusion = f32[2048,128]{1,0:T(8,128)S(1)} fusion(f32[2048,128]{1,0:T(8,128)S(1)} %get-tuple-element.82, s32[12288]{0:T(1024)S(1)} %bitcast.70, f32[12288,128]{1,0:T(8,128)} %fusion.47), kind=kCustom, calls=%fused_computation.5 | custom fusion | flops 1572864 | bytes 18923520 | tf_op jit(solution)/shard_map/scatter-add | solution.py:124
  449.3 2.0 slice_add_fusion.1
  451.4 5.6 %collective-permute-done.11 = bf16[18,34,1,128]{3,2,1,0:T(2,128)(2,1)S(1)} collective-permute-done((bf16[18,34,1,128]{3,2,1,0:T(2,128)(2,1)}, bf16[18,34,1,128]{3,2,1,0:T(2,128)(2,1)S(1)}, u32[]{:S(2)}, u32[]{:S(2)}) %collective-permute-start.11) | collective-permute-done | bytes 156704 | tf_op jit(solution)/shard_map/ppermute | solution.py:16
  457.0 3.4 fusion.30
  460.5 1.5 copy-done.3
  462.0 5.4 %all-reduce.11.cloned.1.call-done = f32[115200]{0:T(1024)} async-done(((f32[115200]{0:T(1024)}), f32[115200]{0:T(1024)}) %all-reduce.11.cloned.1.call-update) | async-done | bytes 460816 | tf_op jit(solution)/shard_map/psum | solution.py:43
  467.5 1.9 slice_add_fusion.3
  469.4 5.3 %scatter-add.58 = f32[16,32,4,128]{3,2,1,0:T(4,128)S(1)} dynamic-update-slice(f32[16,32,4,128]{3,2,1,0:T(4,128)S(1)} %fusion.44, f32[16,32,1,128]{3,2,1,0:T(1,128)S(1)} %slice_add_fusion.3, s32[]{:T(128)} %constant.208.clone.1, s32[]{:T(128)} %constant.208.clone.1, s32[]{:T(128)} %constant.208.clone.1, s32[]{:T(128)} %constant.208.clone.1) | dynamic-update-slice | bytes 524292 | tf_op jit(solution)/shard_map/scatter-add | solution.py:137
  474.7 2.1 slice_add_fusion.2
  476.8 5.3 %scatter-add.59 = f32[16,32,4,128]{3,2,1,0:T(4,128)S(1)} dynamic-update-slice(f32[16,32,4,128]{3,2,1,0:T(4,128)S(1)} %scatter-add.58, f32[16,32,1,128]{3,2,1,0:T(1,128)S(1)} %slice_add_fusion.2, s32[]{:T(128)} %constant.208.clone.1, s32[]{:T(128)} %constant.208.clone.1, s32[]{:T(128)} %constant.219.clone.1, s32[]{:T(128)} %constant.208.clone.1) | dynamic-update-slice | bytes 524292 | tf_op jit(solution)/shard_map/scatter-add | solution.py:137
  482.0 1.0 convert_element_type.87
  483.1 27.1 %all-reduce.13.cloned.1.call-done = f32[115200]{0:T(1024)} async-done(((f32[115200]{0:T(1024)}), f32[115200]{0:T(1024)}) %all-reduce.13.cloned.1.call-update) | async-done | bytes 460816 | tf_op jit(solution)/shard_map/psum | solution.py:43
  510.2 1.7 multiply_reduce_fusion
  512.7 1.1 broadcast_multiply_fusion
  (104 shorter events, 10.7 us)
Async XLA Ops:
  7.2 205.2 %copy-start = (bf16[256,128]{1,0:T(8,128)(2,1)S(1)}, bf16[256,128]{1,0:T(8,128)(2,1)}, u32[]{:S(2)}) copy-start(bf16[256,128]{1,0:T(8,128)(2,1)} %param.33) | copy-start | bytes 196612
  7.2 20.8 %copy-start.2 = (bf16[16,32,4,128]{3,2,1,0:T(4,128)(2,1)S(1)}, bf16[16,32,4,128]{3,2,1,0:T(4,128)(2,1)}, u32[]{:S(2)}) copy-start(bf16[16,32,4,128]{3,2,1,0:T(4,128)(2,1)} %param.25) | copy-start | bytes 1572868
  7.2 460.2 %all-reduce.11.cloned.1.call-start = ((), (), s32[]{:S(2)}) async-start(), calls=%async_computation | async-start | bytes 925696 | tf_op jit(solution)/shard_map/psum | solution.py:43
  8.1 18.3 %collective-permute-start.1 = (bf16[16,1,4,128]{3,2,1,0:T(4,128)(2,1)S(1)}, bf16[16,1,4,128]{3,2,1,0:T(4,128)(2,1)S(1)}, u32[]{:S(2)}, u32[]{:S(2)}) collective-permute-start(bf16[16,1,4,128]{3,2,1,0:T(4,128)(2,1)S(1)} %get-tuple-element.93), channel_id=1, source_target_pairs={{0,4},{4,8},{8,12},{12,16},{16,20},{20,24},{24,28},{28,0},{1,5},{5... | collective-permute-start | bytes 49160 | tf_op jit(solution)/shard_map/ppermute | solution.py:15
  10.2 61.2 %collective-permute-start.4 = (bf16[16,1,4,128]{3,2,1,0:T(4,128)(2,1)S(1)}, bf16[16,1,4,128]{3,2,1,0:T(4,128)(2,1)S(1)}, u32[]{:S(2)}, u32[]{:S(2)}) collective-permute-start(bf16[16,1,4,128]{3,2,1,0:T(4,128)(2,1)S(1)} %get-tuple-element.94), channel_id=1, source_target_pairs={{4,0},{8,4},{12,8},{16,12},{20,16},{24,20},{28,24},{0,28},{5,1},{9... | collective-permute-start | bytes 49160 | tf_op jit(solution)/shard_map/ppermute | solution.py:16
  14.5 56.8 %collective-permute-start.2 = (bf16[1,32,4,128]{3,2,1,0:T(4,128)(2,1)S(1)}, bf16[1,32,4,128]{3,2,1,0:T(4,128)(2,1)S(1)}, u32[]{:S(2)}, u32[]{:S(2)}) collective-permute-start(bf16[1,32,4,128]{3,2,1,0:T(4,128)(2,1)S(1)} %get-tuple-element.89), channel_id=1, source_target_pairs={{0,32},{32,64},{64,96},{96,0},{1,33},{33,65},{65,97},{97,1},{2,34}... | collective-permute-start | bytes 98312 | tf_op jit(solution)/shard_map/ppermute | solution.py:15
  15.9 55.5 %collective-permute-start.3 = (bf16[1,32,4,128]{3,2,1,0:T(4,128)(2,1)S(1)}, bf16[1,32,4,128]{3,2,1,0:T(4,128)(2,1)S(1)}, u32[]{:S(2)}, u32[]{:S(2)}) collective-permute-start(bf16[1,32,4,128]{3,2,1,0:T(4,128)(2,1)S(1)} %get-tuple-element.90), channel_id=1, source_target_pairs={{32,0},{64,32},{96,64},{0,96},{33,1},{65,33},{97,65},{1,97},{34,2}... | collective-permute-start | bytes 98312 | tf_op jit(solution)/shard_map/ppermute | solution.py:16
  19.2 52.2 %collective-permute-start = (bf16[16,32,1,128]{3,2,1,0:T(2,128)(2,1)S(1)}, bf16[16,32,1,128]{3,2,1,0:T(2,128)(2,1)S(1)}, u32[]{:S(2)}, u32[]{:S(2)}) collective-permute-start(bf16[16,32,1,128]{3,2,1,0:T(2,128)(2,1)S(1)} %get-tuple-element.91), channel_id=1, source_target_pairs={{0,1},{1,2},{2,3},{3,0},{4,5},{5,6},{6,7},{7,4},{8,9},{9,10},{10,1... | collective-permute-start | bytes 393224 | tf_op jit(solution)/shard_map/ppermute | solution.py:15
  26.3 45.0 %collective-permute-start.5 = (bf16[16,32,1,128]{3,2,1,0:T(2,128)(2,1)S(1)}, bf16[16,32,1,128]{3,2,1,0:T(2,128)(2,1)S(1)}, u32[]{:S(2)}, u32[]{:S(2)}) collective-permute-start(bf16[16,32,1,128]{3,2,1,0:T(2,128)(2,1)S(1)} %get-tuple-element.92), channel_id=1, source_target_pairs={{1,0},{2,1},{3,2},{0,3},{5,4},{6,5},{7,6},{4,7},{9,8},{10,9},{11,1... | collective-permute-start | bytes 393224 | tf_op jit(solution)/shard_map/ppermute | solution.py:16
  117.5 9.3 %copy-start.12 = (bf16[384,128]{1,0:T(8,128)(2,1)S(1)}, bf16[384,128]{1,0:T(8,128)(2,1)}, u32[]{:S(2)}) copy-start(bf16[384,128]{1,0:T(8,128)(2,1)} %param.29) | copy-start | bytes 294916
  117.5 9.3 %copy-start.17 = (bf16[1,1,1,12288,128]{4,3,2,1,0:T(8,128)(2,1)S(1)}, bf16[1,1,1,12288,128]{4,3,2,1,0:T(8,128)(2,1)}, u32[]{:S(2)}) copy-start(bf16[1,1,1,12288,128]{4,3,2,1,0:T(8,128)(2,1)} %param.26) | copy-start | bytes 9437188
  117.5 9.3 %copy-start.21 = (f32[128]{0:T(128)S(1)}, f32[128]{0:T(128)}, u32[]{:S(2)}) copy-start(f32[128]{0:T(128)} %param.30) | copy-start | bytes 1540
  126.8 3.1 copy-start.4
  126.8 3.1 copy-start.6
  126.8 5.7 %copy-start.20 = (bf16[128,128]{1,0:T(8,128)(2,1)S(1)}, bf16[128,128]{1,0:T(8,128)(2,1)}, u32[]{:S(2)}) copy-start(bf16[128,128]{1,0:T(8,128)(2,1)} %param.31) | copy-start | bytes 98308
  126.8 5.7 %copy-start.22 = (f32[128]{0:T(128)S(1)}, f32[128]{0:T(128)}, u32[]{:S(2)}) copy-start(f32[128]{0:T(128)} %param.32) | copy-start | bytes 1540
  129.8 2.6 copy-start.25
  132.5 3.8 copy-start.10
  132.5 79.9 %copy-start.23 = (f32[128]{0:T(128)S(1)}, f32[128]{0:T(128)}, u32[]{:S(2)}) copy-start(f32[128]{0:T(128)} %param.34) | copy-start | bytes 1540
  136.3 76.6 %copy-start.8 = (bf16[16,32,4,128]{3,2,1,0:T(4,128)(2,1)S(1)}, bf16[16,32,4,128]{3,2,1,0:T(4,128)(2,1)}, u32[]{:S(2)}) copy-start(bf16[16,32,4,128]{3,2,1,0:T(4,128)(2,1)} %param.36) | copy-start | bytes 1572868
  212.4 1.6 copy-start.19
  256.8 14.7 %slice-start = ((s8[6291456]{0:T(1024)(128)(4,1)}), s8[4194304]{0:T(1024)(128)(4,1)S(1)}, s32[]{:S(2)}) async-start(s8[6291456]{0:T(1024)(128)(4,1)} %bitcast.77), calls=%async_computation.2 | async-start | bytes 8388608
  266.1 5.5 %slice-start.1 = ((s8[6291456]{0:T(1024)(128)(4,1)}), s8[2097152]{0:T(1024)(128)(4,1)S(1)}, s32[]{:S(2)}) async-start(s8[6291456]{0:T(1024)(128)(4,1)} %bitcast.77), calls=%async_computation.3 | async-start | bytes 4194304
  271.6 3.3 copy-start.5
  271.6 3.3 copy-start.7
  271.6 3.7 copy-start.18
  356.8 3.9 copy-start.13
  356.8 4.0 copy-start.11
  356.8 4.1 copy-start.24
  356.8 4.1 copy-start.14
  360.8 87.9 %collective-permute-start.7 = (bf16[18,1,6,128]{3,2,1,0:T(8,128)(2,1)S(1)}, bf16[18,1,6,128]{3,2,1,0:T(8,128)(2,1)S(1)}, u32[]{:S(2)}, u32[]{:S(2)}) collective-permute-start(bf16[18,1,6,128]{3,2,1,0:T(8,128)(2,1)S(1)} %get-tuple-element.87), channel_id=1, source_target_pairs={{0,4},{4,8},{8,12},{12,16},{16,20},{20,24},{24,28},{28,0},{1,5},{5... | collective-permute-start | bytes 82952 | tf_op jit(solution)/shard_map/ppermute | solution.py:15
  361.0 0.8 copy-start.9
  361.8 148.4 %all-reduce.13.cloned.1.call-start = ((), (), s32[]{:S(2)}) async-start(), calls=%async_computation.1 | async-start | bytes 925696 | tf_op jit(solution)/shard_map/psum | solution.py:43
  361.8 89.5 %collective-permute-start.10 = (bf16[18,1,6,128]{3,2,1,0:T(8,128)(2,1)S(1)}, bf16[18,1,6,128]{3,2,1,0:T(8,128)(2,1)S(1)}, u32[]{:S(2)}, u32[]{:S(2)}) collective-permute-start(bf16[18,1,6,128]{3,2,1,0:T(8,128)(2,1)S(1)} %get-tuple-element.88), channel_id=1, source_target_pairs={{4,0},{8,4},{12,8},{16,12},{20,16},{24,20},{28,24},{0,28},{5,1},{9... | collective-permute-start | bytes 82952 | tf_op jit(solution)/shard_map/ppermute | solution.py:16
  365.4 85.9 %collective-permute-start.8 = (bf16[1,34,6,128]{3,2,1,0:T(8,128)(2,1)}, bf16[1,34,6,128]{3,2,1,0:T(8,128)(2,1)}, u32[]{:S(2)}, u32[]{:S(2)}) collective-permute-start(bf16[1,34,6,128]{3,2,1,0:T(8,128)(2,1)} %get-tuple-element.83), channel_id=1, source_target_pairs={{0,32},{32,64},{64,96},{96,0},{1,33},{33,65},{65,97},{97,1},{2,34}... | collective-permute-start | bytes 156680 | tf_op jit(solution)/shard_map/ppermute | solution.py:15
  365.6 85.8 %collective-permute-start.9 = (bf16[1,34,6,128]{3,2,1,0:T(8,128)(2,1)}, bf16[1,34,6,128]{3,2,1,0:T(8,128)(2,1)}, u32[]{:S(2)}, u32[]{:S(2)}) collective-permute-start(bf16[1,34,6,128]{3,2,1,0:T(8,128)(2,1)} %get-tuple-element.84), channel_id=1, source_target_pairs={{32,0},{64,32},{96,64},{0,96},{33,1},{65,33},{97,65},{1,97},{34,2}... | collective-permute-start | bytes 156680 | tf_op jit(solution)/shard_map/ppermute | solution.py:16
  368.1 83.3 %collective-permute-start.6 = (bf16[18,34,1,128]{3,2,1,0:T(2,128)(2,1)}, bf16[18,34,1,128]{3,2,1,0:T(2,128)(2,1)}, u32[]{:S(2)}, u32[]{:S(2)}) collective-permute-start(bf16[18,34,1,128]{3,2,1,0:T(2,128)(2,1)} %get-tuple-element.85), channel_id=1, source_target_pairs={{0,1},{1,2},{2,3},{3,0},{4,5},{5,6},{6,7},{7,4},{8,9},{9,10},{10,1... | collective-permute-start | bytes 470024 | tf_op jit(solution)/shard_map/ppermute | solution.py:15
  448.7 0.6 copy-start.15
  448.7 8.3 %collective-permute-start.11 = (bf16[18,34,1,128]{3,2,1,0:T(2,128)(2,1)}, bf16[18,34,1,128]{3,2,1,0:T(2,128)(2,1)S(1)}, u32[]{:S(2)}, u32[]{:S(2)}) collective-permute-start(bf16[18,34,1,128]{3,2,1,0:T(2,128)(2,1)} %get-tuple-element.86), channel_id=1, source_target_pairs={{1,0},{2,1},{3,2},{0,3},{5,4},{6,5},{7,6},{4,7},{9,8},{10,9},{11,1... | collective-permute-start | bytes 470024 | tf_op jit(solution)/shard_map/ppermute | solution.py:16
  449.3 7.7 %copy-start.16 = (bf16[18,1,6,128]{3,2,1,0:T(8,128)(2,1)S(1)}, bf16[18,1,6,128]{3,2,1,0:T(8,128)(2,1)}, u32[]{:S(2)}) copy-start(bf16[18,1,6,128]{3,2,1,0:T(8,128)(2,1)} %copy-done.15) | copy-start | bytes 82948
  460.4 1.6 copy-start.3
  467.5 48.9 %copy-start.1 = (bf16[256,128]{1,0:T(8,128)(2,1)S(1)}, bf16[256,128]{1,0:T(8,128)(2,1)}, u32[]{:S(2)}) copy-start(bf16[256,128]{1,0:T(8,128)(2,1)} %param.33) | copy-start | bytes 196612
Sparse Core Ops, SparseCore 0:
  361.9 105.4 all-reduce.10
  469.8 40.3 all-reduce.12
